TPU v7x, 512 devices: a whole 4x4x16 slice. The times are simulated.
512 devices in a mesh: seq: 128 (over z, y, core), head: 4 (over x).
Axes of the slice: x: 4, y: 4, z: 16, core: 2. Of those that a mesh axis runs over, the one named last changes fastest.
Arguments:
- queries: bfloat16 [65536, 2048], P('seq', 'head'), may hold values from -6 to 6
- key_vectors: bfloat16 [65536, 2048], P('seq', 'head'), may hold values from -6 to 6
- value_vectors: bfloat16 [65536, 2048], P('seq', 'head'), may hold values from -6 to 6
- gate_input: bfloat16 [65536, 2048], P('seq', 'head'), may hold values from -6 to 6
- out_weight: bfloat16 [2048, 4096], P('seq', 'head'), may hold values from -0.125 to 0.125
Outputs:
- layer_output: bfloat16 [65536, 4096], P('seq', 'head')
All inputs are finite; a program needn't handle non-finite values.
Results may differ from a plain program's by a relative error of at most 0.0057.
Values may be sent and summed in bfloat16 or wider, within the bound.
No kernel may reach another device: no remote copies, remote signals or barrier semaphores. Data moves between devices by JAX's collectives and lax.ppermute only.
A program may use at most 64 MiB of HBM per device.

v0:
```python
import jax
import jax.numpy as jnp
from jax import lax
from jax.sharding import Mesh
from jax.sharding import PartitionSpec as P

HD = 128
SEQ = ("seq_0", "seq_1", "seq_2")


def nothing_yet(shard, identity):
    return jnp.broadcast_to(jnp.asarray(identity, shard.dtype), shard.shape)


def carried_in(shard, axes, combine, identity):
    before = start = nothing_yet(shard, identity)
    total = shard
    for axis in reversed(axes):
        count, position = (lax.axis_size(axis), lax.axis_index(axis))
        pieces = lax.all_gather(total, axis)
        inside, total = (start, start)
        for k in range(count):
            passed = k < position
            total = combine(total, pieces[k])
            inside = jnp.where(passed, total, inside)
        before = combine(inside, before)
    return before


def sent_to_all(shard, axis):
    count = lax.axis_size(axis)
    return lax.all_to_all(
        jnp.broadcast_to(shard[None], (count, *shard.shape)), axis, 0, 0, tiled=True
    )


def of_everyone(shard, axis):
    everything = sent_to_all(shard, axis)
    return jnp.sum(everything, axis=0)


def in_order(blocks, dim):
    shape = list(blocks.shape[1:])
    shape[dim] *= blocks.shape[0]
    return jnp.moveaxis(blocks, 0, dim).reshape(shape)


def gather_directly(shard, axis, dim):
    blocks = sent_to_all(shard, axis)
    return in_order(blocks, dim)


def stacked_from(shard, axes, sequence):
    blocks = shard[None]
    for k in sequence:
        blocks = lax.all_gather(blocks, axes[k], axis=0, tiled=True)
    block = [lax.axis_size(axes[k]) for k in reversed(sequence)]
    blocks = blocks.reshape(*block, *shard.shape)
    turned = sorted(range(len(sequence)), key=lambda place: sequence[len(sequence) - 1 - place])
    return blocks.transpose(*turned, *range(len(sequence), blocks.ndim)).reshape(-1, *shard.shape)


def gathered_by_axis(shard, axes, sequence, dim):
    return in_order(stacked_from(shard, axes, sequence), dim)


def add_states(earlier, later):
    return earlier + later


def carried(own_state):
    return carried_in(own_state, SEQ, add_states, jnp.zeros_like(own_state))


def in_shard(qhead, khead, vhead, scale):
    rows = qhead.shape[0]
    step = min(rows, 512)
    scores = jnp.einsum("thd,shd->hts", qhead, khead, preferred_element_type=jnp.float32) * scale
    rowpos = 0 + lax.broadcasted_iota(jnp.int32, (step, step), 0)
    colpos = lax.broadcasted_iota(jnp.int32, (step, step), 1)
    scores = jnp.where((colpos <= rowpos)[None, :, :], scores, 0.0).astype(jnp.bfloat16)
    pieces = jnp.einsum("hts,she->the", scores, vhead, preferred_element_type=jnp.float32)
    return pieces


def per_device(queries, key_vectors, value_vectors, gate_input, out_weight):
    rows, width = queries.shape
    heads = width // HD
    scale = HD ** (-0.5)
    qhead = queries.reshape(rows, heads, HD)
    khead = key_vectors.reshape(rows, heads, HD)
    vhead = value_vectors.reshape(rows, heads, HD)
    own_state = jnp.einsum("thd,the->hde", khead, vhead, preferred_element_type=jnp.float32)
    local = in_shard(qhead, khead, vhead, scale)
    prefix = carried(own_state)
    inter = (
        jnp.einsum(
            "thd,hde->the", qhead, prefix.astype(jnp.bfloat16), preferred_element_type=jnp.float32
        )
        * scale
    )
    attn = (local + inter).reshape(rows, width)
    squares = jnp.sum(attn * attn, axis=1)
    hidden = (attn * jax.nn.silu(gate_input.astype(jnp.float32))).astype(jnp.bfloat16)
    total = of_everyone(squares, "head")
    features = gather_directly(hidden, "head", 1)
    full_block = gathered_by_axis(out_weight, SEQ, (1, 0, 2), 0)
    projected = jnp.dot(features, full_block, preferred_element_type=jnp.float32)
    mean_square = total / features.shape[1]
    return (projected * lax.rsqrt(mean_square + 1e-06)[:, None]).astype(jnp.bfloat16)


def solution(mesh):
    torus = Mesh(
        mesh.devices.reshape(16, 4, 2, mesh.shape["head"]), ("seq_0", "seq_1", "seq_2", "head")
    )
    return jax.shard_map(
        per_device,
        mesh=torus,
        in_specs=(P(SEQ, "head"), P(SEQ, "head"), P(SEQ, "head"), P(SEQ, "head"), P(SEQ, "head")),
        out_specs=P(SEQ, "head"),
        check_vma=False,
    )
```

profile of v0, /device:TPU:8, one launch (start us, length us, event | category | flops | bytes accessed | tf_op | source)
XLA Modules:
  0.0 251.4 jit_solution(18268697951905926214)
XLA Ops:
  6.5 0.0 copy-start
  6.5 0.0 copy-start.3
  6.5 0.0 all-gather.14.cloned.1.call-start
  6.5 1.3 copy.62
  7.9 1.3 fusion.10
  9.2 2.2 all-gather
  11.4 0.7 slice_add_fusion.18
  12.1 0.0 copy-start.1
  12.1 0.0 all-gather.14.cloned.1.call-update
  12.1 0.0 all-gather.10.cloned.1.call-start
  12.2 0.0 copy-done.3
  12.2 15.3 %all-gather.1 = bf16[64,1024]{1,0:T(8,128)(2,1)} all-gather(bf16[16,1024]{1,0:T(8,128)(2,1)S(1)} %copy-done.3), channel_id=3, replica_groups=mesh['seq_0'=16,'seq_1'=4,'seq_2'=2,'head'=4] {'seq_1'}, dimensions={0}, use_global_device_ids=true | all-gather | bytes 163840 | tf_op jit(solution)/shard_map/all_gather | solution.py:56
  27.5 0.0 all-gather.10.cloned.1.call-update
  27.5 0.0 all-gather.8.cloned.1.call-start
  27.6 19.7 %all-gather.14.cloned.1.call-done = f32[16,128,128]{2,1,0:T(8,128)} async-done(((f32[4,128,128]{2,1,0:T(8,128)}), f32[16,128,128]{2,1,0:T(8,128)}) %all-gather.14.cloned.1.call-update) | async-done | bytes 1048592 | tf_op jit(solution)/shard_map/all_gather | solution.py:20
  47.3 1.9 fusion.24
  49.2 0.0 all-gather.8.cloned.1.call-update
  49.3 0.0 copy-start.2
  49.3 0.0 all-gather.12.cloned.1.call-start
  49.3 74.3 %all-gather.10.cloned.1.call-done = bf16[64,16,1024]{2,1,0:T(8,128)(2,1)} async-done(((bf16[4,16,1024]{2,1,0:T(8,128)(2,1)}), bf16[64,16,1024]{2,1,0:T(8,128)(2,1)}) %all-gather.10.cloned.1.call-update) | async-done | bytes 2097168 | tf_op jit(solution)/shard_map/all_gather | solution.py:56
  123.6 0.0 all-gather.12.cloned.1.call-update
  123.7 0.1 iota_compare_fusion
  123.8 76.8 %all-gather.8.cloned.1.call-done = f32[16,4,128,128]{3,2,1,0:T(8,128)} async-done(((f32[1,4,128,128]{3,2,1,0:T(8,128)}), f32[16,4,128,128]{3,2,1,0:T(8,128)}) %all-gather.8.cloned.1.call-update) | async-done | bytes 4194320 | tf_op jit(solution)/shard_map/all_gather | solution.py:20
  200.6 0.0 copy-done
  200.6 0.0 copy-done.1
  200.6 4.0 %fusion.3 = f32[512,4,128]{0,2,1:T(8,128)} fusion(f32[16,4,128,128]{3,2,1,0:T(8,128)} %all-gather.8.cloned.1.call-done, f32[1,4,128,128]{3,2,1,0:T(8,128)} %fusion.24, f32[4,128,128]{2,1,0:T(8,128)S(1)} %copy-done.1, f32[16,128,128]{2,1,0:T(8,128)} %all-gather.14.cloned.1.call-done, f32[8,128,128]{2,1,0:T(8,128)S(1)} %all-gather, pred[]{:T(512)S(6)} %gt.66, ...), kind=kOutput, calls=%fused_computation.6 | convolution fusion | flops 70123520 | bytes 7340054 | tf_op jit(solution)/shard_map/thd,hde->the/dot_general | solution.py:97
  204.6 0.0 copy-done.2
  204.6 2.6 %multiply_reduce_fusion = (f32[512]{0:T(512)S(1)}, f32[512,4,128]{0,2,1:T(8,128)S(1)}) fusion(f32[512,4,128]{0,2,1:T(8,128)} %fusion.3, bf16[512,4,128]{0,2,1:T(8,128)(2,1)S(1)} %bitcast.76, pred[512,512]{1,0:T(8,128)(4,1)S(1)} %iota_compare_fusion, bf16[512,512]{1,0:T(8,128)(2,1)S(1)} %copy-done.2, bf16[512,512]{1,0:T(8,128)(2,1)S(1)} %copy-done), kind=kOutput, calls=%fused_computation.13 | convolution fusion | flops 540802560 | bytes 3934208 | tf_op jit(solution)/shard_map/hts,she->the/dot_general | solution.py:82
  207.2 0.3 copy.56
  207.6 0.6 broadcast_in_dim.37
  208.2 4.3 %all-to-all-start.1 = ((f32[4,1,512]{2,1,0:T(1,128)}), f32[4,1,512]{2,1,0:T(1,128)S(1)}, u32[]{:S(2)}, u32[]{:S(2)}) async-start(f32[4,1,512]{2,1,0:T(1,128)} %broadcast_in_dim.37), calls=%async_computation.1 | async-start | bytes 16384 | tf_op jit(solution)/shard_map/all_to_all | solution.py:32
  212.4 1.4 fusion.8
  213.8 0.2 copy.57
  214.0 3.8 %all-to-all-done.1 = f32[4,1,512]{2,1,0:T(1,128)S(1)} async-done(((f32[4,1,512]{2,1,0:T(1,128)}), f32[4,1,512]{2,1,0:T(1,128)S(1)}, u32[]{:S(2)}, u32[]{:S(2)}) %all-to-all-start.1) | async-done | bytes 8224 | tf_op jit(solution)/shard_map/all_to_all | solution.py:32
  217.8 1.5 broadcast_in_dim.35
  219.3 3.6 %all-to-all-start = ((bf16[4,512,512]{1,2,0:T(8,128)(2,1)}), bf16[4,512,512]{1,2,0:T(8,128)(2,1)S(1)}, u32[]{:S(2)}, u32[]{:S(2)}) async-start(bf16[4,512,512]{1,2,0:T(8,128)(2,1)} %broadcast_in_dim.35), calls=%async_computation | async-start | bytes 4194304 | tf_op jit(solution)/shard_map/all_to_all | solution.py:32
  222.9 0.3 all-gather.12.cloned.1.call-done
  223.2 5.0 %copy.58 = bf16[16,4,2,16,1024]{4,3,2,1,0:T(8,128)(2,1)} copy(bf16[16,4,2,16,1024]{4,3,1,0,2:T(8,128)(2,1)} %bitcast.72) | data formatting | bytes 8388608 | tf_op jit(solution)/shard_map/transpose | solution.py:60
  228.2 11.2 %all-to-all-done = bf16[4,512,512]{1,2,0:T(8,128)(2,1)S(1)} async-done(((bf16[4,512,512]{1,2,0:T(8,128)(2,1)}), bf16[4,512,512]{1,2,0:T(8,128)(2,1)S(1)}, u32[]{:S(2)}, u32[]{:S(2)}) %all-to-all-start) | async-done | bytes 2097184 | tf_op jit(solution)/shard_map/all_to_all | solution.py:32
  239.4 5.5 %multiply_convert_fusion = bf16[512,1024]{1,0:T(8,128)(2,1)} fusion(bf16[512,2048]{0,1:T(8,128)(2,1)S(1)} %bitcast.74, bf16[2048,1024]{1,0:T(8,128)(2,1)} %bitcast.73, f32[512]{0:T(512)S(1)} %add_rsqrt_fusion), kind=kOutput, calls=%fused_computation.1 | convolution fusion | flops 2148532224 | bytes 7342080 | tf_op jit(solution)/shard_map/dot_general | solution.py:108
  (2 shorter events, 0.0 us)
Async XLA Ops:
  6.5 194.1 %copy-start = (bf16[512,512]{1,0:T(8,128)(2,1)S(1)}, bf16[512,512]{1,0:T(8,128)(2,1)}, u32[]{:S(2)}) copy-start(bf16[512,512]{1,0:T(8,128)(2,1)} %param.5) | copy-start | bytes 1572868
  6.5 5.7 %copy-start.3 = (bf16[16,1024]{1,0:T(8,128)(2,1)S(1)}, bf16[16,1024]{1,0:T(8,128)(2,1)}, u32[]{:S(2)}) copy-start(bf16[16,1024]{1,0:T(8,128)(2,1)} %param.9) | copy-start | bytes 98308
  6.5 40.8 %all-gather.14.cloned.1.call-start = ((), (), s32[]{:S(2)}) async-start(), calls=%async_computation.5 | async-start | bytes 1310720 | tf_op jit(solution)/shard_map/all_gather | solution.py:20
  12.1 188.5 %copy-start.1 = (f32[4,128,128]{2,1,0:T(8,128)S(1)}, f32[4,128,128]{2,1,0:T(8,128)}, u32[]{:S(2)}) copy-start(f32[4,128,128]{2,1,0:T(8,128)} %slice_add_fusion.18) | copy-start | bytes 786436
  12.1 111.5 %all-gather.10.cloned.1.call-start = ((), (), s32[]{:S(2)}) async-start(), calls=%async_computation.3 | async-start | bytes 2228224 | tf_op jit(solution)/shard_map/all_gather | solution.py:56
  27.5 173.1 %all-gather.8.cloned.1.call-start = ((), (), s32[]{:S(2)}) async-start(), calls=%async_computation.2 | async-start | bytes 4456448 | tf_op jit(solution)/shard_map/all_gather | solution.py:20
  49.3 155.4 %copy-start.2 = (bf16[512,512]{1,0:T(8,128)(2,1)S(1)}, bf16[512,512]{1,0:T(8,128)(2,1)}, u32[]{:S(2)}) copy-start(bf16[512,512]{1,0:T(8,128)(2,1)} %param.7) | copy-start | bytes 1572868
  49.3 173.9 %all-gather.12.cloned.1.call-start = ((), (), s32[]{:S(2)}) async-start(), calls=%async_computation.4 | async-start | bytes 6291456 | tf_op jit(solution)/shard_map/all_gather | solution.py:56
  208.2 9.6 %all-to-all-start.1 = ((f32[4,1,512]{2,1,0:T(1,128)}), f32[4,1,512]{2,1,0:T(1,128)S(1)}, u32[]{:S(2)}, u32[]{:S(2)}) async-start(f32[4,1,512]{2,1,0:T(1,128)} %broadcast_in_dim.37), calls=%async_computation.1 | async-start | bytes 16384 | tf_op jit(solution)/shard_map/all_to_all | solution.py:32
  219.3 20.1 %all-to-all-start = ((bf16[4,512,512]{1,2,0:T(8,128)(2,1)}), bf16[4,512,512]{1,2,0:T(8,128)(2,1)S(1)}, u32[]{:S(2)}, u32[]{:S(2)}) async-start(bf16[4,512,512]{1,2,0:T(8,128)(2,1)} %broadcast_in_dim.35), calls=%async_computation | async-start | bytes 4194304 | tf_op jit(solution)/shard_map/all_to_all | solution.py:32
Sparse Core Ops, SparseCore 0:
  12.3 34.9 all-gather.13
  49.4 74.1 all-gather.9
  125.7 74.8 all-gather.7
  202.6 20.5 all-gather.11
where the time goes:
time: 252 us; the launch traced here: 251 us
  waiting for transfers between devices  186 us (74%)
  blocking collectives  17.5 us (7%)
  matrix products  13.4 us (5%)
  between operations  13.2 us (5%)
  local copies, waits for them, and re-layouts  8.97 us (4%)
  starting transfers between devices  8 us (3%)
  other arithmetic  4.14 us (2%)
    all_gather x2, waiting for transfers between devices, carried_in(): pieces = lax.all_gather(total, axis)  96.6 us
    all_gather x2, waiting for transfers between devices, stacked_from(): blocks = lax.all_gather(blocks, axes[k], axis=0, tiled=True)  74.5 us
    all_gather x1, blocking collectives, stacked_from(): blocks = lax.all_gather(blocks, axes[k], axis=0, tiled=True)  15.3 us
    all_to_all x2, waiting for transfers between devices, sent_to_all(): lax.all_to_all(jnp.broadcast_to(shard[None], (count, *shard.shape)), axis...  15 us
    all_to_all x2, starting transfers between devices, sent_to_all(): lax.all_to_all(jnp.broadcast_to(shard[None], (count, *shard.shape)), axis...  7.87 us
    dot_general x1, matrix products, per_device(): jnp.dot(features, full_block, preferred_element_type=jnp.float32)  5.51 us
  transfers between devices with their start and end apart: 6, of which 6 were waited for; matrix products, arithmetic and copies ran while one was open for 7% of the time, Pallas kernels for 0%

commit v1 on v0

--- a/solution.py
+++ b/solution.py
@@ -53,7 +53,10 @@
 def stacked_from(shard, axes, sequence):
     blocks = shard[None]
     for k in sequence:
-        blocks = lax.all_gather(blocks, axes[k], axis=0, tiled=True)
+        devices = lax.axis_size(axes[k])
+        tiles = jnp.stack([blocks for _ in range(devices)])
+        tiles = lax.all_to_all(tiles, axes[k], split_axis=0, concat_axis=0)
+        blocks = jnp.concatenate(tiles, axis=0)
     block = [lax.axis_size(axes[k]) for k in reversed(sequence)]
     blocks = blocks.reshape(*block, *shard.shape)
     turned = sorted(range(len(sequence)), key=lambda place: sequence[len(sequence) - 1 - place])

time: 252 us -> 239 us (0.948)
  the two profiles are of different devices: /device:TPU:8 before, /device:TPU:2 now
where the time goes in v1:
time: 239 us
  waiting for transfers between devices  152 us (64%)
  starting transfers between devices  30.8 us (13%)
  matrix products  13.8 us (6%)
  between operations  13.6 us (6%)
  blocking collectives  12.4 us (5%)
  local copies, waits for them, and re-layouts  10.6 us (4%)
  other arithmetic  5.45 us (2%)
    all_to_all x2, waiting for transfers between devices, stacked_from(): tiles = lax.all_to_all(tiles, axes[k], split_axis=0, concat_axis=0)  97.9 us
    all_gather x2, waiting for transfers between devices, carried_in(): pieces = lax.all_gather(total, axis)  37.8 us
    all_to_all x2, starting transfers between devices, stacked_from(): tiles = lax.all_to_all(tiles, axes[k], split_axis=0, concat_axis=0)  20.9 us
    all_to_all x2, waiting for transfers between devices, sent_to_all(): lax.all_to_all(jnp.broadcast_to(shard[None], (count, *shard.shape)), axis...  16.2 us
    all_to_all x1, blocking collectives, stacked_from(): tiles = lax.all_to_all(tiles, axes[k], split_axis=0, concat_axis=0)  10.2 us
    all_to_all x2, starting transfers between devices, sent_to_all(): lax.all_to_all(jnp.broadcast_to(shard[None], (count, *shard.shape)), axis...  9.86 us
    dot_general x1, matrix products, per_device(): jnp.dot(features, full_block, preferred_element_type=jnp.float32)  5.51 us
    all_to_all x1, local copies, waits for them, and re-layouts, stacked_from(): tiles = lax.all_to_all(tiles, axes[k], split_axis=0, concat_axis=0)  5.01 us
  transfers between devices with their start and end apart: 6, of which 5 were waited for; matrix products, arithmetic and copies ran while one was open for 8% of the time, Pallas kernels for 0%

profile of v1, /device:TPU:2, one launch (start us, length us, event | category | flops | bytes accessed | tf_op | source)
XLA Modules:
  0.0 238.8 jit_solution(17685651609442065567)
XLA Ops:
  6.5 0.0 copy-start
  6.5 0.0 copy-start.6
  6.5 0.0 all-gather.7.cloned.1.call-start
  6.5 1.3 copy.52
  7.9 0.0 copy-start.1
  7.9 1.5 fusion.10
  9.4 2.2 all-gather
  11.6 0.7 slice_add_fusion.18
  12.3 0.0 all-gather.7.cloned.1.call-update
  12.3 0.0 copy-done.6
  12.4 10.2 %all_to_all.26 = bf16[4,1,16,1024]{3,2,1,0:T(8,128)(2,1)S(1)} all-to-all(bf16[4,1,16,1024]{3,2,1,0:T(8,128)(2,1)S(1)} %stack.9), channel_id=1, replica_groups=mesh['seq_0'=16,'seq_1'=4,'seq_2'=2,'head'=4] {'seq_1'}, dimensions={0} | all-to-all | bytes 262144 | tf_op jit(solution)/shard_map/all_to_all | solution.py:58
  22.6 1.6 stack.10
  24.2 0.0 copy-done.1
  24.2 15.2 %all-to-all-start.2 = ((bf16[16,4,16,1024]{3,2,1,0:T(8,128)(2,1)}), bf16[16,4,16,1024]{3,2,1,0:T(8,128)(2,1)S(1)}, u32[]{:S(2)}, u32[]{:S(2)}) async-start(bf16[16,4,16,1024]{3,2,1,0:T(8,128)(2,1)} %stack.10), calls=%async_computation.2 | async-start | bytes 4194304 | tf_op jit(solution)/shard_map/all_to_all | solution.py:58
  39.4 0.0 all-gather.5.cloned.1.call-start
  39.5 9.3 %all-gather.7.cloned.1.call-done = f32[16,128,128]{2,1,0:T(8,128)} async-done(((f32[4,128,128]{2,1,0:T(8,128)}), f32[16,128,128]{2,1,0:T(8,128)}) %all-gather.7.cloned.1.call-update) | async-done | bytes 1048592 | tf_op jit(solution)/shard_map/all_gather | solution.py:20
  48.8 2.0 fusion.24
  50.7 0.0 all-gather.5.cloned.1.call-update
  50.8 0.1 iota_compare_fusion
  50.9 97.9 %all-to-all-done.2 = bf16[16,4,16,1024]{3,2,1,0:T(8,128)(2,1)S(1)} async-done(((bf16[16,4,16,1024]{3,2,1,0:T(8,128)(2,1)}), bf16[16,4,16,1024]{3,2,1,0:T(8,128)(2,1)S(1)}, u32[]{:S(2)}, u32[]{:S(2)}) %all-to-all-start.2) | async-done | bytes 2097184 | tf_op jit(solution)/shard_map/all_to_all | solution.py:58
  148.8 2.3 pad_maximum_fusion
  151.1 0.0 copy-start.3
  151.1 0.0 copy-start.4
  151.1 5.7 %all-to-all-start.3 = ((bf16[2,64,16,1024]{3,2,1,0:T(8,128)(2,1)}), bf16[2,64,16,1024]{3,2,1,0:T(8,128)(2,1)}, u32[]{:S(2)}, u32[]{:S(2)}) async-start(bf16[2,64,16,1024]{3,2,1,0:T(8,128)(2,1)} %pad_maximum_fusion), calls=%async_computation.3 | async-start | bytes 8388608 | tf_op jit(solution)/shard_map/all_to_all | solution.py:58
  156.9 0.0 copy-start.2
  156.9 28.5 %all-gather.5.cloned.1.call-done = f32[16,4,128,128]{3,2,1,0:T(8,128)} async-done(((f32[1,4,128,128]{3,2,1,0:T(8,128)}), f32[16,4,128,128]{3,2,1,0:T(8,128)}) %all-gather.5.cloned.1.call-update) | async-done | bytes 4194320 | tf_op jit(solution)/shard_map/all_gather | solution.py:20
  185.4 0.0 copy-done
  185.4 0.0 copy-done.3
  185.4 0.0 copy-done.4
  185.5 4.0 %fusion.3 = f32[512,4,128]{0,2,1:T(8,128)} fusion(f32[16,4,128,128]{3,2,1,0:T(8,128)} %all-gather.5.cloned.1.call-done, f32[1,4,128,128]{3,2,1,0:T(8,128)S(1)} %copy-done.4, f32[4,128,128]{2,1,0:T(8,128)S(1)} %copy-done.3, f32[16,128,128]{2,1,0:T(8,128)} %all-gather.7.cloned.1.call-done, f32[8,128,128]{2,1,0:T(8,128)S(1)} %all-gather, pred[]{:T(512)S(6)} %gt.66, ...), kind=kOutput, calls=%fused_computation.7 | convolution fusion | flops 70123520 | bytes 7340054 | tf_op jit(solution)/shard_map/thd,hde->the/dot_general | solution.py:100
  189.5 0.0 copy-done.2
  189.5 0.0 copy-start.5
  189.5 2.8 %multiply_reduce_fusion = (f32[512]{0:T(512)S(1)}, f32[512,4,128]{0,2,1:T(8,128)S(1)}) fusion(f32[512,4,128]{0,2,1:T(8,128)} %fusion.3, bf16[512,4,128]{0,2,1:T(8,128)(2,1)S(1)} %bitcast.78, pred[512,512]{1,0:T(8,128)(4,1)S(1)} %iota_compare_fusion, bf16[512,512]{1,0:T(8,128)(2,1)} %param.7, bf16[512,512]{1,0:T(8,128)(2,1)S(1)} %copy-done), kind=kOutput, calls=%fused_computation.14 | convolution fusion | flops 540802560 | bytes 3934208 | tf_op jit(solution)/shard_map/hts,she->the/dot_general | solution.py:85
  192.3 0.3 copy.46
  192.6 0.0 all-to-all-done.3
  192.6 0.6 broadcast_in_dim.33
  193.2 4.8 %all-to-all-start.4 = ((f32[4,1,512]{2,1,0:T(1,128)}), f32[4,1,512]{2,1,0:T(1,128)S(1)}, u32[]{:S(2)}, u32[]{:S(2)}) async-start(f32[4,1,512]{2,1,0:T(1,128)} %broadcast_in_dim.33), calls=%async_computation.4 | async-start | bytes 16384 | tf_op jit(solution)/shard_map/all_to_all | solution.py:32
  198.1 0.0 copy-done.5
  198.1 0.3 fusion.8
  198.4 0.2 copy.47
  198.6 3.3 %all-to-all-done.4 = f32[4,1,512]{2,1,0:T(1,128)S(1)} async-done(((f32[4,1,512]{2,1,0:T(1,128)}), f32[4,1,512]{2,1,0:T(1,128)S(1)}, u32[]{:S(2)}, u32[]{:S(2)}) %all-to-all-start.4) | async-done | bytes 8224 | tf_op jit(solution)/shard_map/all_to_all | solution.py:32
  201.9 1.5 broadcast_in_dim.32
  203.4 5.0 %all-to-all-start = ((bf16[4,512,512]{1,2,0:T(8,128)(2,1)}), bf16[4,512,512]{1,2,0:T(8,128)(2,1)S(1)}, u32[]{:S(2)}, u32[]{:S(2)}) async-start(bf16[4,512,512]{1,2,0:T(8,128)(2,1)} %broadcast_in_dim.32), calls=%async_computation | async-start | bytes 4194304 | tf_op jit(solution)/shard_map/all_to_all | solution.py:32
  208.5 5.0 %copy.48 = bf16[2,64,16,1024]{3,2,0,1:T(8,128)(2,1)} copy(bf16[2,64,16,1024]{3,2,1,0:T(8,128)(2,1)} %all-to-all-done.3) | data formatting | bytes 8388608 | tf_op jit(solution)/shard_map/all_to_all | solution.py:58
  213.5 12.9 %all-to-all-done = bf16[4,512,512]{1,2,0:T(8,128)(2,1)S(1)} async-done(((bf16[4,512,512]{1,2,0:T(8,128)(2,1)}), bf16[4,512,512]{1,2,0:T(8,128)(2,1)S(1)}, u32[]{:S(2)}, u32[]{:S(2)}) %all-to-all-start) | async-done | bytes 2097184 | tf_op jit(solution)/shard_map/all_to_all | solution.py:32
  226.4 5.5 %multiply_convert_fusion = bf16[512,1024]{1,0:T(8,128)(2,1)} fusion(bf16[512,2048]{0,1:T(8,128)(2,1)S(1)} %bitcast.76, bf16[2048,1024]{1,0:T(8,128)(2,1)} %bitcast.75, f32[512]{0:T(512)S(1)} %add_rsqrt_fusion), kind=kOutput, calls=%fused_computation.2 | convolution fusion | flops 2148532224 | bytes 7342080 | tf_op jit(solution)/shard_map/dot_general | solution.py:111
  (3 shorter events, 0.0 us)
Async XLA Ops:
  6.5 178.9 %copy-start = (bf16[512,512]{1,0:T(8,128)(2,1)S(1)}, bf16[512,512]{1,0:T(8,128)(2,1)}, u32[]{:S(2)}) copy-start(bf16[512,512]{1,0:T(8,128)(2,1)} %param.5) | copy-start | bytes 1572868
  6.5 5.8 %copy-start.6 = (bf16[16,1024]{1,0:T(8,128)(2,1)S(1)}, bf16[16,1024]{1,0:T(8,128)(2,1)}, u32[]{:S(2)}) copy-start(bf16[16,1024]{1,0:T(8,128)(2,1)} %param.9) | copy-start | bytes 98308
  6.5 42.2 %all-gather.7.cloned.1.call-start = ((), (), s32[]{:S(2)}) async-start(), calls=%async_computation.6 | async-start | bytes 1310720 | tf_op jit(solution)/shard_map/all_gather | solution.py:20
  7.9 16.3 %copy-start.1 = (bf16[512,512]{0,1:T(8,128)(2,1)}, bf16[512,512]{0,1:T(8,128)(2,1)S(1)}, u32[]{:S(2)}) copy-start(bf16[512,512]{0,1:T(8,128)(2,1)S(1)} %copy.52) | copy-start | bytes 1572868
  24.2 124.6 %all-to-all-start.2 = ((bf16[16,4,16,1024]{3,2,1,0:T(8,128)(2,1)}), bf16[16,4,16,1024]{3,2,1,0:T(8,128)(2,1)S(1)}, u32[]{:S(2)}, u32[]{:S(2)}) async-start(bf16[16,4,16,1024]{3,2,1,0:T(8,128)(2,1)} %stack.10), calls=%async_computation.2 | async-start | bytes 4194304 | tf_op jit(solution)/shard_map/all_to_all | solution.py:58
  39.4 146.0 %all-gather.5.cloned.1.call-start = ((), (), s32[]{:S(2)}) async-start(), calls=%async_computation.5 | async-start | bytes 4456448 | tf_op jit(solution)/shard_map/all_gather | solution.py:20
  151.1 34.3 %copy-start.3 = (f32[4,128,128]{2,1,0:T(8,128)S(1)}, f32[4,128,128]{2,1,0:T(8,128)}, u32[]{:S(2)}) copy-start(f32[4,128,128]{2,1,0:T(8,128)} %slice_add_fusion.18) | copy-start | bytes 786436
  151.1 34.3 %copy-start.4 = (f32[1,4,128,128]{3,2,1,0:T(8,128)S(1)}, f32[1,4,128,128]{3,2,1,0:T(8,128)}, u32[]{:S(2)}) copy-start(f32[1,4,128,128]{3,2,1,0:T(8,128)} %fusion.24) | copy-start | bytes 786436
  151.1 41.5 %all-to-all-start.3 = ((bf16[2,64,16,1024]{3,2,1,0:T(8,128)(2,1)}), bf16[2,64,16,1024]{3,2,1,0:T(8,128)(2,1)}, u32[]{:S(2)}, u32[]{:S(2)}) async-start(bf16[2,64,16,1024]{3,2,1,0:T(8,128)(2,1)} %pad_maximum_fusion), calls=%async_computation.3 | async-start | bytes 8388608 | tf_op jit(solution)/shard_map/all_to_all | solution.py:58
  156.9 32.6 %copy-start.2 = (bf16[512,512]{0,1:T(8,128)(2,1)S(1)}, bf16[512,512]{0,1:T(8,128)(2,1)}, u32[]{:S(2)}) copy-start(bf16[512,512]{0,1:T(8,128)(2,1)} %copy-done.1) | copy-start | bytes 1572868
  189.5 8.6 %copy-start.5 = (bf16[512,512]{1,0:T(8,128)(2,1)S(1)}, bf16[512,512]{1,0:T(8,128)(2,1)}, u32[]{:S(2)}) copy-start(bf16[512,512]{1,0:T(8,128)(2,1)} %param.8) | copy-start | bytes 1572868
  193.2 8.7 %all-to-all-start.4 = ((f32[4,1,512]{2,1,0:T(1,128)}), f32[4,1,512]{2,1,0:T(1,128)S(1)}, u32[]{:S(2)}, u32[]{:S(2)}) async-start(f32[4,1,512]{2,1,0:T(1,128)} %broadcast_in_dim.33), calls=%async_computation.4 | async-start | bytes 16384 | tf_op jit(solution)/shard_map/all_to_all | solution.py:32
  203.4 23.0 %all-to-all-start = ((bf16[4,512,512]{1,2,0:T(8,128)(2,1)}), bf16[4,512,512]{1,2,0:T(8,128)(2,1)S(1)}, u32[]{:S(2)}, u32[]{:S(2)}) async-start(bf16[4,512,512]{1,2,0:T(8,128)(2,1)} %broadcast_in_dim.32), calls=%async_computation | async-start | bytes 4194304 | tf_op jit(solution)/shard_map/all_to_all | solution.py:32
Sparse Core Ops, SparseCore 0:
  12.5 36.2 all-gather.6
  50.9 134.5 all-gather.4
